TPU v7x, 32 devices: a whole 2x2x4 slice. The times are simulated.
32 devices in a mesh: pipe: 2 (over x), dp: 8 (over z, y), tensor: 2 (over core).
Axes of the slice: x: 2, y: 2, z: 4, core: 2. Of those that a mesh axis runs over, the one named last changes fastest.
Arguments:
- inputs: bfloat16 [2, 8, 256, 1536], P(None, 'dp'), may hold values from -6 to 6
- cotangents: bfloat16 [2, 8, 256, 1536], P(None, 'dp'), may hold values from -6 to 6
- norm_scales: float32 [2, 1536, 2], P('pipe'), may hold values from 0.5 to 1.5
- w_query: bfloat16 [2, 1536, 1536], P('pipe', None, 'tensor'), may hold values from -0.15625 to 0.15625
- key_weight: bfloat16 [2, 1536, 768], P('pipe', None, 'tensor'), may hold values from -0.15625 to 0.15625
- value_weight: bfloat16 [2, 1536, 768], P('pipe', None, 'tensor'), may hold values from -0.15625 to 0.15625
- w_out: bfloat16 [2, 1536, 1536], P('pipe', None, 'tensor'), may hold values from -0.875 to 0.875
- w_gate: bfloat16 [2, 1536, 4096], P('pipe', None, 'tensor'), may hold values from -0.15625 to 0.15625
- w_up: bfloat16 [2, 1536, 4096], P('pipe', None, 'tensor'), may hold values from -0.15625 to 0.15625
- down_weight: bfloat16 [2, 1536, 4096], P('pipe', None, 'tensor'), may hold values from -0.09375 to 0.09375
Outputs:
- section_out: bfloat16 [2, 2, 8, 256, 1536], P('pipe', None, 'dp')
- section_in_grad: bfloat16 [2, 2, 8, 256, 1536], P('pipe', None, 'dp')
- grad_scales: float32 [2, 1536, 2], P('pipe', 'dp')
- grad_query: float32 [2, 1536, 1536], P('pipe', 'dp', 'tensor')
- grad_key: float32 [2, 1536, 768], P('pipe', 'dp', 'tensor')
- value_weight_gradient: float32 [2, 1536, 768], P('pipe', 'dp', 'tensor')
- grad_out: float32 [2, 1536, 1536], P('pipe', 'dp', 'tensor')
- grad_gate: float32 [2, 1536, 4096], P('pipe', 'dp', 'tensor')
- grad_up: float32 [2, 1536, 4096], P('pipe', 'dp', 'tensor')
- grad_down: float32 [2, 1536, 4096], P('pipe', 'dp', 'tensor')
All inputs are finite; a program needn't handle non-finite values.
Results may differ from a plain program's by a relative error of at most 0.03.
Values may be sent and summed in bfloat16 or wider, within the bound.
A program may use at most 256 MiB of HBM per device.

v0:
```python
import jax
import jax.numpy as jnp
from jax import lax
from jax.sharding import PartitionSpec as P

HEAD_SIZE = 96
EPS = 1e-05
THETA = 100000.0


def passed_along(value, axis, by):
    peers = lax.axis_size(axis)
    pairs = [(i, i + by) for i in range(peers) if 0 <= i + by < peers]
    return lax.ppermute(value, axis, pairs)


def rope_tables(length, size):
    positions = jnp.arange(length, dtype=jnp.float32)
    freqs = THETA ** (-(jnp.arange(size // 2, dtype=jnp.float32) * 2.0 / size))
    angles = positions[:, None] * freqs[None, :]
    cosine = jnp.concatenate([jnp.cos(angles), jnp.cos(angles)], axis=-1)
    sine = jnp.concatenate([jnp.sin(angles), jnp.sin(angles)], axis=-1)
    return (cosine[:, None, :], sine[:, None, :])


def rotate(values, cosine, sine):
    half = values.shape[-1] // 2
    turned = jnp.concatenate([-values[..., half:], values[..., :half]], axis=-1)
    return values * cosine + turned * sine


def rotate_back(grads, cosine, sine):
    half = grads.shape[-1] // 2
    moved = grads * sine
    turned = jnp.concatenate([moved[..., half:], -moved[..., :half]], axis=-1)
    return grads * cosine + turned


def times_t(left, right):
    return lax.dot_general(
        left, right, (((1,), (1,)), ((), ())), preferred_element_type=jnp.float32
    )


def over_rows(left, right):
    return lax.dot_general(
        left, right, (((0,), (0,)), ((), ())), preferred_element_type=jnp.float32
    )


def heads_total(partial_value):
    return lax.psum(partial_value.astype(jnp.bfloat16), "tensor").astype(jnp.float32)


def inputs_total(partial_value):
    return lax.psum(partial_value.astype(jnp.bfloat16), "tensor").astype(jnp.float32)


def norm_rows(values, gain):
    scale = lax.rsqrt(jnp.mean(values * values, axis=-1, keepdims=True) + EPS)
    return (scale, (values * scale * gain).astype(jnp.bfloat16))


def score_table(query, keys):
    length = query.shape[0]
    scores = jnp.einsum(
        "qgrd,kgd->grqk", query, keys, preferred_element_type=jnp.float32
    ) * HEAD_SIZE ** (-0.5)
    causal = jnp.arange(length)[:, None] >= jnp.arange(length)[None, :]
    return (scores, causal)


def forward_layer(hidden, params):
    scales, w_query, key_weight, value_weight, w_out, w_gate, w_up, down_weight = params
    length = hidden.shape[0]
    groups = key_weight.shape[1] // HEAD_SIZE
    wide = hidden.astype(jnp.float32)
    scale_one, normed_one = norm_rows(wide, scales[:, 0])
    cosine, sine = rope_tables(length, HEAD_SIZE)
    query = (
        rotate(
            jnp.dot(normed_one, w_query, preferred_element_type=jnp.float32).reshape(
                length, -1, HEAD_SIZE
            ),
            cosine,
            sine,
        )
        .astype(jnp.bfloat16)
        .reshape(length, groups, -1, HEAD_SIZE)
    )
    keys = rotate(
        jnp.dot(normed_one, key_weight, preferred_element_type=jnp.float32).reshape(
            length, groups, HEAD_SIZE
        ),
        cosine,
        sine,
    ).astype(jnp.bfloat16)
    values = (
        jnp.dot(normed_one, value_weight, preferred_element_type=jnp.float32)
        .astype(jnp.bfloat16)
        .reshape(length, groups, HEAD_SIZE)
    )
    scores, causal = score_table(query, keys)
    log_total = jnp.log(jnp.sum(jnp.where(causal, jnp.exp(scores), 0.0), axis=-1))
    probs = jnp.where(causal, jnp.exp(scores - log_total[..., None]), 0.0).astype(jnp.bfloat16)
    mixed = (
        jnp.einsum("grqk,kgd->qgrd", probs, values, preferred_element_type=jnp.float32)
        .astype(jnp.bfloat16)
        .reshape(length, -1)
    )
    middle = wide + heads_total(times_t(mixed, w_out))
    scale_two, normed_two = norm_rows(middle, scales[:, 1])
    gate = jnp.dot(normed_two, w_gate, preferred_element_type=jnp.float32)
    upward = jnp.dot(normed_two, w_up, preferred_element_type=jnp.float32)
    activated = (gate * jax.nn.sigmoid(gate) * upward).astype(jnp.bfloat16)
    result = (middle + heads_total(times_t(activated, down_weight))).astype(jnp.bfloat16)
    record = (
        hidden,
        scale_one,
        normed_one,
        query,
        keys,
        values,
        mixed,
        log_total,
        middle,
        scale_two,
        normed_two,
        gate,
        upward,
        activated,
    )
    return (record, result)


def backward_feedforward(record, cotangent, params):
    (
        hidden,
        scale_one,
        normed_one,
        query,
        keys,
        values,
        mixed,
        log_total,
        middle,
        scale_two,
        normed_two,
        gate,
        upward,
        activated,
    ) = record
    scales, w_query, key_weight, value_weight, w_out, w_gate, w_up, down_weight = params
    grad_down = over_rows(cotangent, activated)
    d_act = jnp.dot(cotangent, down_weight, preferred_element_type=jnp.float32)
    sig = jax.nn.sigmoid(gate)
    d_gate = (d_act * upward * sig * (1.0 + gate * (1.0 - sig))).astype(jnp.bfloat16)
    d_up = (d_act * gate * sig).astype(jnp.bfloat16)
    grad_gate = over_rows(normed_two, d_gate)
    grad_up = over_rows(normed_two, d_up)
    d_normed = inputs_total(times_t(d_gate, w_gate) + times_t(d_up, w_up))
    weighted = d_normed * scales[:, 1]
    gain_two = jnp.sum(d_normed * middle * scale_two, axis=0)
    d_middle = (
        cotangent.astype(jnp.float32)
        + scale_two * weighted
        - middle * scale_two**3 * jnp.mean(weighted * middle, axis=-1, keepdims=True)
    )
    return (d_middle, (grad_gate, grad_up, grad_down, gain_two))


def backward_attention(record, d_middle, params):
    (
        hidden,
        scale_one,
        normed_one,
        query,
        keys,
        values,
        mixed,
        log_total,
        middle,
        scale_two,
        normed_two,
        gate,
        upward,
        activated,
    ) = record
    scales, w_query, key_weight, value_weight, w_out, w_gate, w_up, down_weight = params
    length = hidden.shape[0]
    groups = keys.shape[1]
    d_mid_low = d_middle.astype(jnp.bfloat16)
    grad_out = over_rows(d_mid_low, mixed)
    d_mixed = jnp.dot(d_mid_low, w_out, preferred_element_type=jnp.float32).astype(jnp.bfloat16)
    d_heads = d_mixed.reshape(length, groups, -1, HEAD_SIZE)
    scores, causal = score_table(query, keys)
    probs = jnp.where(causal, jnp.exp(scores - log_total[..., None]), 0.0)
    d_probs = jnp.einsum("qgrd,kgd->grqk", d_heads, values, preferred_element_type=jnp.float32)
    d_values = jnp.einsum(
        "grqk,qgrd->kgd", probs.astype(jnp.bfloat16), d_heads, preferred_element_type=jnp.float32
    )
    delta = jnp.sum(
        d_heads.astype(jnp.float32)
        * mixed.reshape(length, groups, -1, HEAD_SIZE).astype(jnp.float32),
        axis=-1,
    )
    d_scores = (
        probs * (d_probs - jnp.transpose(delta, (1, 2, 0))[..., None]) * HEAD_SIZE ** (-0.5)
    ).astype(jnp.bfloat16)
    cosine, sine = rope_tables(length, HEAD_SIZE)
    d_query = (
        rotate_back(
            jnp.einsum(
                "grqk,kgd->qgrd", d_scores, keys, preferred_element_type=jnp.float32
            ).reshape(length, -1, HEAD_SIZE),
            cosine,
            sine,
        )
        .astype(jnp.bfloat16)
        .reshape(length, -1)
    )
    d_keys = (
        rotate_back(
            jnp.einsum("grqk,qgrd->kgd", d_scores, query, preferred_element_type=jnp.float32),
            cosine,
            sine,
        )
        .astype(jnp.bfloat16)
        .reshape(length, -1)
    )
    d_vals = d_values.astype(jnp.bfloat16).reshape(length, -1)
    grad_query = over_rows(normed_one, d_query)
    grad_key = over_rows(normed_one, d_keys)
    value_weight_gradient = over_rows(normed_one, d_vals)
    d_first = inputs_total(
        times_t(d_query, w_query) + times_t(d_keys, key_weight) + times_t(d_vals, value_weight)
    )
    weighted_one = d_first * scales[:, 0]
    wide = hidden.astype(jnp.float32)
    gain_one = jnp.sum(d_first * wide * scale_one, axis=0)
    d_hidden = (
        d_middle
        + scale_one * weighted_one
        - wide * scale_one**3 * jnp.mean(weighted_one * wide, axis=-1, keepdims=True)
    ).astype(jnp.bfloat16)
    return (d_hidden, (grad_query, grad_key, value_weight_gradient, grad_out, gain_one))


def body(
    inputs,
    cotangents,
    norm_scales,
    w_query,
    key_weight,
    value_weight,
    w_out,
    w_gate,
    w_up,
    down_weight,
):
    params = (
        norm_scales[0],
        w_query[0],
        key_weight[0],
        value_weight[0],
        w_out[0],
        w_gate[0],
        w_up[0],
        down_weight[0],
    )
    section_index = lax.axis_index("pipe")
    is_first = section_index == 0
    micros = inputs.shape[0]
    length = inputs.shape[2]
    width = inputs.shape[3]
    incoming = jnp.zeros((length, width), jnp.bfloat16)
    saved = []
    results = []
    for step_index in range(micros + 1):
        own_input = inputs[min(step_index, micros - 1), 0]
        record, result = forward_layer(jnp.where(is_first, own_input, incoming), params)
        saved.append(record)
        results.append(result)
        if step_index < micros:
            incoming = passed_along(result, "pipe", 1)
    stacked = jax.tree.map(lambda *entries: jnp.stack(entries), *saved)
    returned = jnp.zeros((length, width), jnp.bfloat16)
    in_grads = []
    for step_index in range(micros + 1):
        micro_index = step_index - 1 + section_index
        weight_mask = jnp.logical_and(micro_index >= 0, micro_index < micros).astype(jnp.float32)
        slot_index = jnp.clip(micro_index + section_index, 0, micros)
        record = jax.tree.map(
            lambda entry: lax.dynamic_index_in_dim(entry, slot_index, 0, keepdims=False), stacked
        )
        cotangent = jnp.where(is_first, returned, cotangents[min(step_index, micros - 1), 0])
        d_middle, ffn_part = backward_feedforward(record, cotangent, params)
        if step_index == 0:
            ffn_sums = jax.tree.map(lambda extra: weight_mask * extra, ffn_part)
        else:
            ffn_sums = jax.tree.map(
                lambda total, extra: total + weight_mask * extra, ffn_sums, ffn_part
            )
        d_hidden, attn_part = backward_attention(record, d_middle, params)
        if step_index == 0:
            attn_sums = jax.tree.map(lambda extra: weight_mask * extra, attn_part)
        else:
            attn_sums = jax.tree.map(
                lambda total, extra: total + weight_mask * extra, attn_sums, attn_part
            )
        in_grads.append(d_hidden)
        if step_index < micros:
            returned = passed_along(d_hidden, "pipe", -1)
    gain_grads = jnp.stack([attn_sums[4], ffn_sums[3]], axis=1)[None]
    shards = (
        lax.psum_scatter(
            attn_sums[0][None].astype(jnp.bfloat16), "dp", scatter_dimension=1, tiled=True
        ).astype(jnp.float32),
        lax.psum_scatter(
            attn_sums[1][None].astype(jnp.bfloat16), "dp", scatter_dimension=1, tiled=True
        ).astype(jnp.float32),
        lax.psum_scatter(
            attn_sums[2][None].astype(jnp.bfloat16), "dp", scatter_dimension=1, tiled=True
        ).astype(jnp.float32),
        lax.psum_scatter(
            attn_sums[3][None].astype(jnp.bfloat16), "dp", scatter_dimension=1, tiled=True
        ).astype(jnp.float32),
        lax.psum_scatter(
            ffn_sums[0][None].astype(jnp.bfloat16), "dp", scatter_dimension=1, tiled=True
        ).astype(jnp.float32),
        lax.psum_scatter(
            ffn_sums[1][None].astype(jnp.bfloat16), "dp", scatter_dimension=1, tiled=True
        ).astype(jnp.float32),
        lax.psum_scatter(
            ffn_sums[2][None].astype(jnp.bfloat16), "dp", scatter_dimension=1, tiled=True
        ).astype(jnp.float32),
        lax.psum_scatter(
            gain_grads.astype(jnp.bfloat16), "dp", scatter_dimension=1, tiled=True
        ).astype(jnp.float32),
    )
    (
        grad_query,
        grad_key,
        value_weight_gradient,
        grad_out,
        grad_gate,
        grad_up,
        grad_down,
        grad_scales,
    ) = shards
    section_out = lax.dynamic_slice_in_dim(jnp.stack(results), section_index, micros, 0).reshape(
        1, micros, 1, length, width
    )
    section_in_grad = lax.dynamic_slice_in_dim(
        jnp.stack(in_grads), 1 - section_index, micros, 0
    ).reshape(1, micros, 1, length, width)
    return (
        section_out,
        section_in_grad,
        grad_scales,
        grad_query,
        grad_key,
        value_weight_gradient,
        grad_out,
        grad_gate,
        grad_up,
        grad_down,
    )


def solution(mesh):
    placed = (
        P(None, "dp", None, None),
        P(None, "dp", None, None),
        P("pipe", None, None),
        P("pipe", None, "tensor"),
        P("pipe", None, "tensor"),
        P("pipe", None, "tensor"),
        P("pipe", None, "tensor"),
        P("pipe", None, "tensor"),
        P("pipe", None, "tensor"),
        P("pipe", None, "tensor"),
    )
    return jax.shard_map(
        body,
        mesh=mesh,
        in_specs=placed,
        out_specs=(
            P("pipe", None, "dp", None, None),
            P("pipe", None, "dp", None, None),
            P("pipe", "dp", None),
            P("pipe", "dp", "tensor"),
            P("pipe", "dp", "tensor"),
            P("pipe", "dp", "tensor"),
            P("pipe", "dp", "tensor"),
            P("pipe", "dp", "tensor"),
            P("pipe", "dp", "tensor"),
            P("pipe", "dp", "tensor"),
        ),
        check_vma=False,
    )
```

profile of v0, /device:TPU:0, one launch (start us, length us, event | category | flops | bytes accessed | tf_op | source)
XLA Modules:
  0.0 1268.2 jit_solution(18007858066272877327)
XLA Ops:
  32.4 21.8 %all-reduce.13.cloned.1.call-done = bf16[256,1536]{1,0:T(8,128)(2,1)} async-done(((bf16[256,1536]{1,0:T(8,128)(2,1)}), bf16[256,1536]{1,0:T(8,128)(2,1)}) %all-reduce.13.cloned.1.call-update) | async-done | bytes 786448 | tf_op jit(solution)/shard_map/psum | solution.py:52
  71.2 20.3 %all-reduce.15.cloned.1.call-done = bf16[256,1536]{1,0:T(8,128)(2,1)} async-done(((bf16[256,1536]{1,0:T(8,128)(2,1)}), bf16[256,1536]{1,0:T(8,128)(2,1)}) %all-reduce.15.cloned.1.call-update) | async-done | bytes 786448 | tf_op jit(solution)/shard_map/psum | solution.py:52
  97.9 16.7 %collective-permute-done = bf16[256,1536]{1,0:T(8,128)(2,1)S(1)} collective-permute-done((bf16[256,1536]{1,0:T(8,128)(2,1)S(1)}, bf16[256,1536]{1,0:T(8,128)(2,1)S(1)}, u32[]{:S(2)}, u32[]{:S(2)}) %collective-permute-start) | collective-permute-done | bytes 786464 | tf_op jit(solution)/shard_map/ppermute | solution.py:14
  128.9 21.0 %all-reduce.17.cloned.1.call-done = bf16[256,1536]{1,0:T(8,128)(2,1)} async-done(((bf16[256,1536]{1,0:T(8,128)(2,1)}), bf16[256,1536]{1,0:T(8,128)(2,1)}) %all-reduce.17.cloned.1.call-update) | async-done | bytes 786448 | tf_op jit(solution)/shard_map/psum | solution.py:52
  165.5 20.3 %all-reduce.19.cloned.1.call-done = bf16[256,1536]{1,0:T(8,128)(2,1)} async-done(((bf16[256,1536]{1,0:T(8,128)(2,1)}), bf16[256,1536]{1,0:T(8,128)(2,1)}) %all-reduce.19.cloned.1.call-update) | async-done | bytes 786448 | tf_op jit(solution)/shard_map/psum | solution.py:52
  193.4 16.6 %collective-permute-done.1 = bf16[256,1536]{1,0:T(8,128)(2,1)} collective-permute-done((bf16[256,1536]{1,0:T(8,128)(2,1)}, bf16[256,1536]{1,0:T(8,128)(2,1)}, u32[]{:S(2)}, u32[]{:S(2)}) %collective-permute-start.1) | collective-permute-done | bytes 786464 | tf_op jit(solution)/shard_map/ppermute | solution.py:14
  235.1 11.6 all-reduce.21.cloned.1.call-done
  263.1 7.5 fusion.132
  283.9 14.7 %all-reduce.23.cloned.1.call-done = bf16[256,1536]{1,0:T(8,128)(2,1)} async-done(((bf16[256,1536]{1,0:T(8,128)(2,1)}), bf16[256,1536]{1,0:T(8,128)(2,1)}) %all-reduce.23.cloned.1.call-update) | async-done | bytes 786448 | tf_op jit(solution)/shard_map/psum | solution.py:56
  324.6 16.6 %all-reduce.25.cloned.1.call-done = bf16[256,1536]{1,0:T(8,128)(2,1)} async-done(((bf16[256,1536]{1,0:T(8,128)(2,1)}), bf16[256,1536]{1,0:T(8,128)(2,1)}) %all-reduce.25.cloned.1.call-update) | async-done | bytes 786448 | tf_op jit(solution)/shard_map/psum | solution.py:56
  347.8 20.0 %collective-permute-done.2 = bf16[256,1536]{1,0:T(8,128)(2,1)S(1)} collective-permute-done((bf16[256,1536]{1,0:T(8,128)(2,1)S(1)}, bf16[256,1536]{1,0:T(8,128)(2,1)S(1)}, u32[]{:S(2)}, u32[]{:S(2)}) %collective-permute-start.2) | collective-permute-done | bytes 786464 | tf_op jit(solution)/shard_map/ppermute | solution.py:14
  367.9 6.6 fusion.118
  382.6 16.1 %all-reduce.27.cloned.1.call-done = bf16[256,1536]{1,0:T(8,128)(2,1)} async-done(((bf16[256,1536]{1,0:T(8,128)(2,1)}), bf16[256,1536]{1,0:T(8,128)(2,1)}) %all-reduce.27.cloned.1.call-update) | async-done | bytes 786448 | tf_op jit(solution)/shard_map/psum | solution.py:56
  422.3 18.9 %all-reduce.29.cloned.1.call-done = bf16[256,1536]{1,0:T(8,128)(2,1)} async-done(((bf16[256,1536]{1,0:T(8,128)(2,1)}), bf16[256,1536]{1,0:T(8,128)(2,1)}) %all-reduce.29.cloned.1.call-update) | async-done | bytes 786448 | tf_op jit(solution)/shard_map/psum | solution.py:56
  450.3 17.2 %collective-permute-done.3 = bf16[256,1536]{1,0:T(8,128)(2,1)S(1)} collective-permute-done((bf16[256,1536]{1,0:T(8,128)(2,1)S(1)}, bf16[256,1536]{1,0:T(8,128)(2,1)S(1)}, u32[]{:S(2)}, u32[]{:S(2)}) %collective-permute-start.3) | collective-permute-done | bytes 786464 | tf_op jit(solution)/shard_map/ppermute | solution.py:14
  467.6 6.6 fusion.104
  492.5 12.1 all-reduce.31.cloned.1.call-done
  529.3 19.4 %all-reduce.33.cloned.1.call-done = (bf16[256,1536]{1,0:T(8,128)(2,1)}, bf16[256,1536]{1,0:T(8,128)(2,1)}) async-done(((bf16[256,1536]{1,0:T(8,128)(2,1)}, bf16[256,1536]{1,0:T(8,128)(2,1)}), (bf16[256,1536]{1,0:T(8,128)(2,1)}, bf16[256,1536]{1,0:T(8,128)(2,1)})) %all-reduce.33.cloned.1.call-update) | async-done | bytes 1572880 | tf_op jit(solution)/shard_map/psum | solution.py:52
  590.9 6.5 fusion.296
  597.4 12.5 fusion
  611.1 7.7 fusion.298
  618.8 6.5 fusion.294
  625.3 12.6 fusion.1
  647.6 6.5 fusion.256
  654.2 12.6 fusion.2
  674.1 11.2 reduce-scatter.13.cloned.1.call-done
  686.9 65.5 %reduce-scatter.15.cloned.1.call-done = bf16[1,192,384]{2,1,0:T(8,128)(2,1)} async-done(((bf16[1,1536,384]{2,1,0:T(8,128)(2,1)}), bf16[1,192,384]{2,1,0:T(8,128)(2,1)}) %reduce-scatter.15.cloned.1.call-update) | async-done | bytes 147472 | tf_op jit(solution)/shard_map/reduce_scatter | solution.py:322
  754.1 70.3 %reduce-scatter.17.cloned.1.call-done = bf16[1,192,768]{2,1,0:T(8,128)(2,1)} async-done(((bf16[1,1536,768]{2,1,0:T(8,128)(2,1)}), bf16[1,192,768]{2,1,0:T(8,128)(2,1)}) %reduce-scatter.17.cloned.1.call-update) | async-done | bytes 294928 | tf_op jit(solution)/shard_map/reduce_scatter | solution.py:325
  826.2 70.4 %reduce-scatter.11.cloned.1.call-done = bf16[1,192,768]{2,1,0:T(8,128)(2,1)} async-done(((bf16[1,1536,768]{2,1,0:T(8,128)(2,1)}), bf16[1,192,768]{2,1,0:T(8,128)(2,1)}) %reduce-scatter.11.cloned.1.call-update) | async-done | bytes 294928 | tf_op jit(solution)/shard_map/reduce_scatter | solution.py:316
  898.4 118.9 %reduce-scatter.19.cloned.1.call-done = bf16[1,192,2048]{2,1,0:T(8,128)(2,1)} async-done(((bf16[1,1536,2048]{2,1,0:T(8,128)(2,1)}), bf16[1,192,2048]{2,1,0:T(8,128)(2,1)}) %reduce-scatter.19.cloned.1.call-update) | async-done | bytes 786448 | tf_op jit(solution)/shard_map/reduce_scatter | solution.py:328
  1019.8 118.3 %reduce-scatter.21.cloned.1.call-done = bf16[1,192,2048]{2,1,0:T(8,128)(2,1)} async-done(((bf16[1,1536,2048]{2,1,0:T(8,128)(2,1)}), bf16[1,192,2048]{2,1,0:T(8,128)(2,1)}) %reduce-scatter.21.cloned.1.call-update) | async-done | bytes 786448 | tf_op jit(solution)/shard_map/reduce_scatter | solution.py:331
  1140.5 118.4 %reduce-scatter.23.cloned.1.call-done = bf16[1,192,2048]{2,1,0:T(8,128)(2,1)} async-done(((bf16[1,1536,2048]{2,1,0:T(8,128)(2,1)}), bf16[1,192,2048]{2,1,0:T(8,128)(2,1)}) %reduce-scatter.23.cloned.1.call-update) | async-done | bytes 786448 | tf_op jit(solution)/shard_map/reduce_scatter | solution.py:334
  (618 shorter events, 329.9 us)
Async XLA Ops:
  7.2 23.4 %copy-start = (bf16[1,1536,768]{2,1,0:T(8,128)(2,1)S(1)}, bf16[1,1536,768]{2,1,0:T(8,128)(2,1)}, u32[]{:S(2)}) copy-start(bf16[1,1536,768]{2,1,0:T(8,128)(2,1)} %param.16) | copy-start | bytes 7077892
  7.2 47.0 %all-reduce.13.cloned.1.call-start = ((), (), s32[]{:S(2)}) async-start(), calls=%async_computation.8 | async-start | bytes 1572864 | tf_op jit(solution)/shard_map/psum | solution.py:52
  32.3 59.2 %all-reduce.15.cloned.1.call-start = ((), (), s32[]{:S(2)}) async-start(), calls=%async_computation.9 | async-start | bytes 1572864 | tf_op jit(solution)/shard_map/psum | solution.py:52
  71.2 78.7 %all-reduce.17.cloned.1.call-start = ((), (), s32[]{:S(2)}) async-start(), calls=%async_computation.10 | async-start | bytes 1572864 | tf_op jit(solution)/shard_map/psum | solution.py:52
  91.5 23.4 %copy-start.24 = (bf16[1,1536,384]{2,1,0:T(8,128)(2,1)S(1)}, bf16[1,1536,384]{2,1,0:T(8,128)(2,1)}, u32[]{:S(2)}) copy-start(bf16[1,1536,384]{2,1,0:T(8,128)(2,1)} %param.15) | copy-start | bytes 3538948
  93.4 21.1 %collective-permute-start = (bf16[256,1536]{1,0:T(8,128)(2,1)S(1)}, bf16[256,1536]{1,0:T(8,128)(2,1)S(1)}, u32[]{:S(2)}, u32[]{:S(2)}) collective-permute-start(bf16[256,1536]{1,0:T(8,128)(2,1)S(1)} %add_convert_fusion.7), channel_id=1, source_target_pairs={{0,16},{1,17},{2,18},{3,19},{4,20},{5,21},{6,22},{7,23},{8,24},{9,... | collective-permute-start | bytes 2359304 | tf_op jit(solution)/shard_map/ppermute | solution.py:14
  114.9 70.9 %copy-start.18 = (bf16[256,1536]{1,0:T(8,128)(2,1)}, bf16[256,1536]{1,0:T(8,128)(2,1)S(1)}, u32[]{:S(2)}) copy-start(bf16[256,1536]{1,0:T(8,128)(2,1)S(1)} %get-tuple-element.29) | copy-start | bytes 2359300
  128.8 57.0 %all-reduce.19.cloned.1.call-start = ((), (), s32[]{:S(2)}) async-start(), calls=%async_computation.11 | async-start | bytes 1572864 | tf_op jit(solution)/shard_map/psum | solution.py:52
  165.5 81.2 %all-reduce.21.cloned.1.call-start = ((), (), s32[]{:S(2)}) async-start(), calls=%async_computation.12 | async-start | bytes 1572864 | tf_op jit(solution)/shard_map/psum | solution.py:52
  188.8 21.2 %collective-permute-start.1 = (bf16[256,1536]{1,0:T(8,128)(2,1)}, bf16[256,1536]{1,0:T(8,128)(2,1)}, u32[]{:S(2)}, u32[]{:S(2)}) collective-permute-start(bf16[256,1536]{1,0:T(8,128)(2,1)} %get-tuple-element.46), channel_id=1, source_target_pairs={{0,16},{1,17},{2,18},{3,19},{4,20},{5,21},{6,22},{7,23},{8,24},{9,... | collective-permute-start | bytes 2359304 | tf_op jit(solution)/shard_map/ppermute | solution.py:14
  225.4 73.2 %all-reduce.23.cloned.1.call-start = ((), (), s32[]{:S(2)}) async-start(), calls=%async_computation.13 | async-start | bytes 1572864 | tf_op jit(solution)/shard_map/psum | solution.py:56
  278.2 63.0 %all-reduce.25.cloned.1.call-start = ((), (), s32[]{:S(2)}) async-start(), calls=%async_computation.14 | async-start | bytes 1572864 | tf_op jit(solution)/shard_map/psum | solution.py:56
  320.9 77.8 %all-reduce.27.cloned.1.call-start = ((), (), s32[]{:S(2)}) async-start(), calls=%async_computation.15 | async-start | bytes 1572864 | tf_op jit(solution)/shard_map/psum | solution.py:56
  343.8 24.1 %copy-start.43 = (bf16[2,1,256,1536]{3,2,1,0:T(8,128)(2,1)S(1)}, bf16[2,1,256,1536]{3,2,1,0:T(8,128)(2,1)}, u32[]{:S(2)}) copy-start(bf16[2,1,256,1536]{3,2,1,0:T(8,128)(2,1)} %param.11) | copy-start | bytes 4718596
  343.8 30.8 %slice-start.6 = ((s8[6291456]{0:T(1024)(128)(4,1)}), s8[4194304]{0:T(1024)(128)(4,1)S(1)}, s32[]{:S(2)}) async-start(s8[6291456]{0:T(1024)(128)(4,1)} %bitcast.922), calls=%async_computation.33 | async-start | bytes 8388608
  343.8 32.8 %slice-start.8 = ((s8[6291456]{0:T(1024)(128)(4,1)}), s8[4194304]{0:T(1024)(128)(4,1)S(1)}, s32[]{:S(2)}) async-start(s8[6291456]{0:T(1024)(128)(4,1)} %bitcast.924), calls=%async_computation.35 | async-start | bytes 8388608
  345.8 22.0 %collective-permute-start.2 = (bf16[256,1536]{1,0:T(8,128)(2,1)S(1)}, bf16[256,1536]{1,0:T(8,128)(2,1)S(1)}, u32[]{:S(2)}, u32[]{:S(2)}) collective-permute-start(bf16[256,1536]{1,0:T(8,128)(2,1)S(1)} %fusion.176), channel_id=1, source_target_pairs={{16,0},{17,1},{18,2},{19,3},{20,4},{21,5},{22,6},{23,7},{24,8},{25... | collective-permute-start | bytes 2359304 | tf_op jit(solution)/shard_map/ppermute | solution.py:14
  379.4 61.9 %all-reduce.29.cloned.1.call-start = ((), (), s32[]{:S(2)}) async-start(), calls=%async_computation.16 | async-start | bytes 1572864 | tf_op jit(solution)/shard_map/psum | solution.py:56
  420.9 83.7 %all-reduce.31.cloned.1.call-start = ((), (), s32[]{:S(2)}) async-start(), calls=%async_computation.17 | async-start | bytes 1572864 | tf_op jit(solution)/shard_map/psum | solution.py:56
  445.8 21.7 %collective-permute-start.3 = (bf16[256,1536]{1,0:T(8,128)(2,1)S(1)}, bf16[256,1536]{1,0:T(8,128)(2,1)S(1)}, u32[]{:S(2)}, u32[]{:S(2)}) collective-permute-start(bf16[256,1536]{1,0:T(8,128)(2,1)S(1)} %fusion.170), channel_id=1, source_target_pairs={{16,0},{17,1},{18,2},{19,3},{20,4},{21,5},{22,6},{23,7},{24,8},{25... | collective-permute-start | bytes 2359304 | tf_op jit(solution)/shard_map/ppermute | solution.py:14
  485.2 63.5 %all-reduce.33.cloned.1.call-start = ((), (), s32[]{:S(2)}) async-start(), calls=%async_computation.26 | async-start | bytes 3145728 | tf_op jit(solution)/shard_map/psum | solution.py:52
  526.9 23.7 %copy-start.146 = (f32[1536]{0:T(1024)S(1)}, f32[1536]{0:T(1024)}, u32[]{:S(2)}) copy-start(f32[1536]{0:T(1024)} %get-tuple-element.16) | copy-start | bytes 18436
  526.9 23.7 %copy-start.148 = (f32[1536]{0:T(1024)S(1)}, f32[1536]{0:T(1024)}, u32[]{:S(2)}) copy-start(f32[1536]{0:T(1024)} %get-tuple-element.18) | copy-start | bytes 18436
  526.9 145.7 %reduce-scatter.25.cloned.1.call-start = ((), (), s32[]{:S(2)}) async-start(), calls=%async_computation.25 | async-start | bytes 442368
  529.3 25.2 %copy-start.158 = (f32[256]{0:T(256)S(1)}, f32[256]{0:T(256)}, u32[]{:S(2)}) copy-start(f32[256]{0:T(256)} %copy-done.156) | copy-start | bytes 3076
  554.4 130.9 %reduce-scatter.13.cloned.1.call-start = ((), (), s32[]{:S(2)}) async-start(), calls=%async_computation.19 | async-start | bytes 1327104 | tf_op jit(solution)/shard_map/reduce_scatter | solution.py:319
  563.3 189.2 %reduce-scatter.15.cloned.1.call-start = ((), (), s32[]{:S(2)}) async-start(), calls=%async_computation.20 | async-start | bytes 1327104 | tf_op jit(solution)/shard_map/reduce_scatter | solution.py:322
  568.1 256.3 %reduce-scatter.17.cloned.1.call-start = ((), (), s32[]{:S(2)}) async-start(), calls=%async_computation.21 | async-start | bytes 2654208 | tf_op jit(solution)/shard_map/reduce_scatter | solution.py:325
  574.8 321.7 %reduce-scatter.11.cloned.1.call-start = ((), (), s32[]{:S(2)}) async-start(), calls=%async_computation.18 | async-start | bytes 2654208 | tf_op jit(solution)/shard_map/reduce_scatter | solution.py:316
  581.6 435.7 %reduce-scatter.19.cloned.1.call-start = ((), (), s32[]{:S(2)}) async-start(), calls=%async_computation.22 | async-start | bytes 7077888 | tf_op jit(solution)/shard_map/reduce_scatter | solution.py:328
  609.9 528.2 %reduce-scatter.21.cloned.1.call-start = ((), (), s32[]{:S(2)}) async-start(), calls=%async_computation.23 | async-start | bytes 7077888 | tf_op jit(solution)/shard_map/reduce_scatter | solution.py:331
  637.9 621.1 %reduce-scatter.23.cloned.1.call-start = ((), (), s32[]{:S(2)}) async-start(), calls=%async_computation.24 | async-start | bytes 7077888 | tf_op jit(solution)/shard_map/reduce_scatter | solution.py:334
  (174 other events, 665.5 us)
Sparse Core Ops, SparseCore 0:
  32.5 21.6 all-reduce.12
  71.3 20.1 all-reduce.14
  128.9 20.8 all-reduce.16
  165.6 20.1 all-reduce.18
  225.5 21.1 all-reduce.20
  278.4 20.1 all-reduce.22
  321.0 20.1 all-reduce.24
  379.5 19.1 all-reduce.26
  421.0 20.1 all-reduce.28
  485.3 19.2 all-reduce.30
  527.0 21.6 all-reduce.32
  554.5 63.3 reduce-scatter.24
  621.4 63.8 reduce-scatter.12
  688.5 63.8 reduce-scatter.14
  755.8 68.5 reduce-scatter.16
  827.7 68.8 reduce-scatter.10
  900.0 117.2 reduce-scatter.18
  1020.8 117.2 reduce-scatter.20
  1141.7 117.2 reduce-scatter.22
where the time goes:
time: 1280 us; the launch traced here: 1270 us
  waiting for transfers between devices  837 us (65%)
  matrix products  240 us (19%)
  other arithmetic  105 us (8%)
  local copies, waits for them, and re-layouts  55.1 us (4%)
  between operations  16.5 us (1%)
  starting transfers between devices  14.8 us (1%)
    reduce_scatter x1, waiting for transfers between devices, body(): lax.psum_scatter(ffn_sums[0][None].astype(jnp.bfloat16), 'dp', scatter_di...  119 us
    reduce_scatter x1, waiting for transfers between devices, body(): lax.psum_scatter(ffn_sums[2][None].astype(jnp.bfloat16), 'dp', scatter_di...  118 us
    reduce_scatter x1, waiting for transfers between devices, body(): lax.psum_scatter(ffn_sums[1][None].astype(jnp.bfloat16), 'dp', scatter_di...  118 us
    psum x6, waiting for transfers between devices, heads_total(): lax.psum(partial_value.astype(jnp.bfloat16), 'tensor').astype(jnp.float32)  114 us
    dot_general x21, matrix products, over_rows(): lax.dot_general(left, right, (((0,), (0,)), ((), ())), preferred_element_...  96.3 us
    psum x5, waiting for transfers between devices, inputs_total(): lax.psum(partial_value.astype(jnp.bfloat16), 'tensor').astype(jnp.float32)  78.4 us
    ppermute x4, waiting for transfers between devices, passed_along(): return lax.ppermute(value, axis, pairs)  70.5 us
    reduce_scatter x1, waiting for transfers between devices, body(): lax.psum_scatter(attn_sums[0][None].astype(jnp.bfloat16), 'dp', scatter_d...  70.4 us
  transfers between devices with their start and end apart: 23, of which 22 were waited for; matrix products, arithmetic and copies ran while one was open for 12% of the time, Pallas kernels for 0%

commit v1 on v0

--- a/solution.py
+++ b/solution.py
@@ -49,7 +49,9 @@
 
 
 def heads_total(partial_value):
-    return lax.psum(partial_value.astype(jnp.bfloat16), "tensor").astype(jnp.float32)
+    return jnp.sum(lax.all_gather(partial_value.astype(jnp.bfloat16), "tensor"), axis=0).astype(
+        jnp.float32
+    )
 
 
 def inputs_total(partial_value):

time: 1280 us -> 1240 us (0.969)
  waiting for transfers between devices: 837 us -> 773 us
  other arithmetic: 105 us -> 118 us
    psum x6 -> x0, waiting for transfers between devices: 114 us -> none  [heads_total(): lax.psum(partial_value.astype(jnp.bfloat16), 'tensor').astype(jnp.float32)]
    all_gather x0 -> x6, waiting for transfers between devices: none -> 36.4 us  [heads_total(): lax.all_gather(partial_value.astype(jnp.bfloat16), 'tensor')]
    reduce_sum x0 -> x6, other arithmetic: none -> 15.6 us  [heads_total(): jnp.sum(lax.all_gather(partial_value.astype(jnp.bfloat16), 'tensor'), axi...]
    psum x5 -> x6, waiting for transfers between devices: 78.4 us -> 86.6 us  [inputs_total(): lax.psum(partial_value.astype(jnp.bfloat16), 'tensor').astype(jnp.float32)]
    another operation x19 -> x18, other arithmetic: 29.5 us -> 24.9 us  [body(): stacked = jax.tree.map(lambda *entries: jnp.stack(entries), *saved)]
    unnamed x372 -> x390, local copies, waits for them, and re-layouts: 39.3 us -> 39.5 us
  transfers between devices with their start and end apart: 23 -> 24, of which waited for: 22 -> 21; matrix products, arithmetic and copies ran while one was open for 12% -> 15% of each run, Pallas kernels for 0% -> 0%
where the time goes in v1:
time: 1240 us; the launch traced here: 1230 us
  waiting for transfers between devices  773 us (62%)
  matrix products  245 us (20%)
  other arithmetic  118 us (10%)
  local copies, waits for them, and re-layouts  54.3 us (4%)
  starting transfers between devices  25.2 us (2%)
  between operations  17.2 us (1%)
    reduce_scatter x1, waiting for transfers between devices, body(): lax.psum_scatter(ffn_sums[0][None].astype(jnp.bfloat16), 'dp', scatter_di...  119 us
    reduce_scatter x1, waiting for transfers between devices, body(): lax.psum_scatter(ffn_sums[1][None].astype(jnp.bfloat16), 'dp', scatter_di...  118 us
    reduce_scatter x1, waiting for transfers between devices, body(): lax.psum_scatter(ffn_sums[2][None].astype(jnp.bfloat16), 'dp', scatter_di...  118 us
    dot_general x21, matrix products, over_rows(): lax.dot_general(left, right, (((0,), (0,)), ((), ())), preferred_element_...  102 us
    psum x6, waiting for transfers between devices, inputs_total(): lax.psum(partial_value.astype(jnp.bfloat16), 'tensor').astype(jnp.float32)  86.6 us
    ppermute x4, waiting for transfers between devices, passed_along(): return lax.ppermute(value, axis, pairs)  74.5 us
    reduce_scatter x1, waiting for transfers between devices, body(): lax.psum_scatter(attn_sums[3][None].astype(jnp.bfloat16), 'dp', scatter_d...  70.4 us
    reduce_scatter x1, waiting for transfers between devices, body(): lax.psum_scatter(attn_sums[0][None].astype(jnp.bfloat16), 'dp', scatter_d...  70.3 us
  transfers between devices with their start and end apart: 24, of which 21 were waited for; matrix products, arithmetic and copies ran while one was open for 15% of the time, Pallas kernels for 0%

profile of v1, /device:TPU:0, one launch (start us, length us, event | category | flops | bytes accessed | tf_op | source)
XLA Modules:
  0.0 1232.6 jit_solution(2559118250470027013)
XLA Ops:
  32.4 12.6 %all-gather.13.cloned.1.call-done = bf16[512,1536]{1,0:T(8,128)(2,1)} async-done(((bf16[256,1536]{1,0:T(8,128)(2,1)}), bf16[512,1536]{1,0:T(8,128)(2,1)}) %all-gather.13.cloned.1.call-update) | async-done | bytes 1572880 | tf_op jit(solution)/shard_map/all_gather | solution.py:52
  61.1 11.7 all-gather.17.cloned.1.call-start
  81.3 17.2 %collective-permute-done = bf16[256,1536]{1,0:T(8,128)(2,1)S(1)} collective-permute-done((bf16[256,1536]{1,0:T(8,128)(2,1)S(1)}, bf16[256,1536]{1,0:T(8,128)(2,1)S(1)}, u32[]{:S(2)}, u32[]{:S(2)}) %collective-permute-start) | collective-permute-done | bytes 786464 | tf_op jit(solution)/shard_map/ppermute | solution.py:14
  112.8 11.8 all-gather.17.cloned.1.call-done
  143.0 11.1 all-gather.19.cloned.1.call-done
  164.4 16.7 %collective-permute-done.1 = bf16[256,1536]{1,0:T(8,128)(2,1)} collective-permute-done((bf16[256,1536]{1,0:T(8,128)(2,1)}, bf16[256,1536]{1,0:T(8,128)(2,1)}, u32[]{:S(2)}, u32[]{:S(2)}) %collective-permute-start.1) | collective-permute-done | bytes 786464 | tf_op jit(solution)/shard_map/ppermute | solution.py:14
  255.2 8.9 all-reduce.7.cloned.1.call-done
  293.0 14.0 %all-reduce.9.cloned.1.call-done = bf16[256,1536]{1,0:T(8,128)(2,1)} async-done(((bf16[256,1536]{1,0:T(8,128)(2,1)}), bf16[256,1536]{1,0:T(8,128)(2,1)}) %all-reduce.9.cloned.1.call-update) | async-done | bytes 786448 | tf_op jit(solution)/shard_map/psum | solution.py:58
  315.2 20.1 %collective-permute-done.2 = bf16[256,1536]{1,0:T(8,128)(2,1)S(1)} collective-permute-done((bf16[256,1536]{1,0:T(8,128)(2,1)S(1)}, bf16[256,1536]{1,0:T(8,128)(2,1)S(1)}, u32[]{:S(2)}, u32[]{:S(2)}) %collective-permute-start.2) | collective-permute-done | bytes 786464 | tf_op jit(solution)/shard_map/ppermute | solution.py:14
  335.4 6.6 fusion.118
  350.0 16.2 %all-reduce.11.cloned.1.call-done = bf16[256,1536]{1,0:T(8,128)(2,1)} async-done(((bf16[256,1536]{1,0:T(8,128)(2,1)}), bf16[256,1536]{1,0:T(8,128)(2,1)}) %all-reduce.11.cloned.1.call-update) | async-done | bytes 786448 | tf_op jit(solution)/shard_map/psum | solution.py:58
  388.1 18.7 %all-reduce.13.cloned.1.call-done = bf16[256,1536]{1,0:T(8,128)(2,1)} async-done(((bf16[256,1536]{1,0:T(8,128)(2,1)}), bf16[256,1536]{1,0:T(8,128)(2,1)}) %all-reduce.13.cloned.1.call-update) | async-done | bytes 786448 | tf_op jit(solution)/shard_map/psum | solution.py:58
  413.4 20.6 %collective-permute-done.3 = bf16[256,1536]{1,0:T(8,128)(2,1)} collective-permute-done((bf16[256,1536]{1,0:T(8,128)(2,1)}, bf16[256,1536]{1,0:T(8,128)(2,1)}, u32[]{:S(2)}, u32[]{:S(2)}) %collective-permute-start.3) | collective-permute-done | bytes 786464 | tf_op jit(solution)/shard_map/ppermute | solution.py:14
  435.5 6.6 fusion.104
  458.8 13.7 %all-reduce.15.cloned.1.call-done = bf16[256,1536]{1,0:T(8,128)(2,1)} async-done(((bf16[256,1536]{1,0:T(8,128)(2,1)}), bf16[256,1536]{1,0:T(8,128)(2,1)}) %all-reduce.15.cloned.1.call-update) | async-done | bytes 786448 | tf_op jit(solution)/shard_map/psum | solution.py:58
  499.6 15.1 %all-reduce.17.cloned.1.call-done = bf16[256,1536]{1,0:T(8,128)(2,1)} async-done(((bf16[256,1536]{1,0:T(8,128)(2,1)}), bf16[256,1536]{1,0:T(8,128)(2,1)}) %all-reduce.17.cloned.1.call-update) | async-done | bytes 786448 | tf_op jit(solution)/shard_map/psum | solution.py:58
  543.1 6.4 fusion.307
  549.5 6.5 fusion.303
  556.0 12.5 %fusion = bf16[1,1536,2048]{2,1,0:T(8,128)(2,1)} fusion(bf16[256,2048]{1,0:T(8,128)(2,1)S(1)} %copy-done.124, f32[1536,2048]{1,0:T(8,128)} %fusion.303, f32[1536,2048]{1,0:T(8,128)} %fusion.307, f32[]{:T(128)S(6)} %convert_element_type.703, f32[]{:T(128)S(6)} %convert_element_type.702, f32[]{:T(128)S(6)} %convert_element_type.701, ...), kind=kOutput, calls=%fused_computation.3 | convolution fusion | flops 1629487104 | bytes 33292304 | tf_op jit(solution)/shard_map/dot_general | solution.py:46
  569.7 7.7 fusion.305
  577.4 6.5 fusion.301
  583.9 12.5 %fusion.1 = bf16[1,1536,2048]{2,1,0:T(8,128)(2,1)} fusion(bf16[256,2048]{1,0:T(8,128)(2,1)S(1)} %copy-done.122, f32[1536,2048]{1,0:T(8,128)} %fusion.301, f32[1536,2048]{1,0:T(8,128)} %fusion.305, f32[]{:T(128)S(6)} %convert_element_type.703, f32[]{:T(128)S(6)} %convert_element_type.702, f32[]{:T(128)S(6)} %convert_element_type.701, ...), kind=kOutput, calls=%fused_computation.4 | convolution fusion | flops 1629487104 | bytes 33292304 | tf_op jit(solution)/shard_map/dot_general | solution.py:46
  599.7 6.4 fusion.264
  606.1 6.5 fusion.262
  612.6 12.6 %fusion.2 = bf16[1,1536,2048]{2,1,0:T(8,128)(2,1)} fusion(bf16[256,1536]{1,0:T(8,128)(2,1)S(1)} %copy-done.43, f32[1536,2048]{1,0:T(8,128)} %fusion.262, f32[1536,2048]{1,0:T(8,128)} %fusion.264, f32[]{:T(128)S(6)} %convert_element_type.703, f32[]{:T(128)S(6)} %convert_element_type.702, f32[]{:T(128)S(6)} %convert_element_type.701, ...), kind=kOutput, calls=%fused_computation.5 | convolution fusion | flops 1629487104 | bytes 33292304 | tf_op jit(solution)/shard_map/dot_general | solution.py:46
  636.1 13.1 %reduce-scatter.13.cloned.1.call-done = bf16[1,192,384]{2,1,0:T(8,128)(2,1)} async-done(((bf16[1,1536,384]{2,1,0:T(8,128)(2,1)}), bf16[1,192,384]{2,1,0:T(8,128)(2,1)}) %reduce-scatter.13.cloned.1.call-update) | async-done | bytes 147472 | tf_op jit(solution)/shard_map/reduce_scatter | solution.py:321
  650.9 65.5 %reduce-scatter.15.cloned.1.call-done = bf16[1,192,384]{2,1,0:T(8,128)(2,1)} async-done(((bf16[1,1536,384]{2,1,0:T(8,128)(2,1)}), bf16[1,192,384]{2,1,0:T(8,128)(2,1)}) %reduce-scatter.15.cloned.1.call-update) | async-done | bytes 147472 | tf_op jit(solution)/shard_map/reduce_scatter | solution.py:324
  718.0 70.3 %reduce-scatter.11.cloned.1.call-done = bf16[1,192,768]{2,1,0:T(8,128)(2,1)} async-done(((bf16[1,1536,768]{2,1,0:T(8,128)(2,1)}), bf16[1,192,768]{2,1,0:T(8,128)(2,1)}) %reduce-scatter.11.cloned.1.call-update) | async-done | bytes 294928 | tf_op jit(solution)/shard_map/reduce_scatter | solution.py:318
  790.1 70.4 %reduce-scatter.17.cloned.1.call-done = bf16[1,192,768]{2,1,0:T(8,128)(2,1)} async-done(((bf16[1,1536,768]{2,1,0:T(8,128)(2,1)}), bf16[1,192,768]{2,1,0:T(8,128)(2,1)}) %reduce-scatter.17.cloned.1.call-update) | async-done | bytes 294928 | tf_op jit(solution)/shard_map/reduce_scatter | solution.py:327
  862.3 118.9 %reduce-scatter.19.cloned.1.call-done = bf16[1,192,2048]{2,1,0:T(8,128)(2,1)} async-done(((bf16[1,1536,2048]{2,1,0:T(8,128)(2,1)}), bf16[1,192,2048]{2,1,0:T(8,128)(2,1)}) %reduce-scatter.19.cloned.1.call-update) | async-done | bytes 786448 | tf_op jit(solution)/shard_map/reduce_scatter | solution.py:330
  983.7 118.4 %reduce-scatter.21.cloned.1.call-done = bf16[1,192,2048]{2,1,0:T(8,128)(2,1)} async-done(((bf16[1,1536,2048]{2,1,0:T(8,128)(2,1)}), bf16[1,192,2048]{2,1,0:T(8,128)(2,1)}) %reduce-scatter.21.cloned.1.call-update) | async-done | bytes 786448 | tf_op jit(solution)/shard_map/reduce_scatter | solution.py:333
  1104.6 118.3 %reduce-scatter.23.cloned.1.call-done = bf16[1,192,2048]{2,1,0:T(8,128)(2,1)} async-done(((bf16[1,1536,2048]{2,1,0:T(8,128)(2,1)}), bf16[1,192,2048]{2,1,0:T(8,128)(2,1)}) %reduce-scatter.23.cloned.1.call-update) | async-done | bytes 786448 | tf_op jit(solution)/shard_map/reduce_scatter | solution.py:336
  (645 shorter events, 341.3 us)
Async XLA Ops:
  7.2 37.8 %all-gather.13.cloned.1.call-start = ((), (), s32[]{:S(2)}) async-start(), calls=%async_computation.21 | async-start | bytes 2359296 | tf_op jit(solution)/shard_map/all_gather | solution.py:52
  27.3 353.1 %copy-start.26 = (f32[256,96]{0,1:T(8,128)}, f32[256,96]{0,1:T(8,128)S(1)}, u32[]{:S(2)}) copy-start(f32[256,96]{0,1:T(8,128)S(1)} %get-tuple-element.110) | copy-start | bytes 294916
  27.3 353.3 %copy-start.23 = (f32[256,96]{0,1:T(8,128)}, f32[256,96]{0,1:T(8,128)S(1)}, u32[]{:S(2)}) copy-start(f32[256,96]{0,1:T(8,128)S(1)} %get-tuple-element.109) | copy-start | bytes 294916
  32.4 40.5 %all-gather.15.cloned.1.call-start = ((), (), s32[]{:S(2)}) async-start(), calls=%async_computation.22 | async-start | bytes 2359296 | tf_op jit(solution)/shard_map/all_gather | solution.py:52
  46.7 28.8 %copy-start.28 = (bf16[256,1536]{1,0:T(8,128)(2,1)}, bf16[256,1536]{1,0:T(8,128)(2,1)S(1)}, u32[]{:S(2)}) copy-start(bf16[256,1536]{1,0:T(8,128)(2,1)S(1)} %reduce_sum.290) | copy-start | bytes 2359300
  61.1 63.6 %all-gather.17.cloned.1.call-start = ((), (), s32[]{:S(2)}) async-start(), calls=%async_computation.23 | async-start | bytes 2359296 | tf_op jit(solution)/shard_map/all_gather | solution.py:52
  77.5 21.0 %collective-permute-start = (bf16[256,1536]{1,0:T(8,128)(2,1)S(1)}, bf16[256,1536]{1,0:T(8,128)(2,1)S(1)}, u32[]{:S(2)}, u32[]{:S(2)}) collective-permute-start(bf16[256,1536]{1,0:T(8,128)(2,1)S(1)} %fusion.189), channel_id=1, source_target_pairs={{0,16},{1,17},{2,18},{3,19},{4,20},{5,21},{6,22},{7,23},{8,24},{9,... | collective-permute-start | bytes 2359304 | tf_op jit(solution)/shard_map/ppermute | solution.py:14
  98.8 58.1 %copy-start.16 = (bf16[256,1536]{1,0:T(8,128)(2,1)}, bf16[256,1536]{1,0:T(8,128)(2,1)S(1)}, u32[]{:S(2)}) copy-start(bf16[256,1536]{1,0:T(8,128)(2,1)S(1)} %get-tuple-element.27) | copy-start | bytes 2359300
  112.7 41.4 %all-gather.19.cloned.1.call-start = ((), (), s32[]{:S(2)}) async-start(), calls=%async_computation.24 | async-start | bytes 2359296 | tf_op jit(solution)/shard_map/all_gather | solution.py:52
  143.0 65.6 %all-gather.21.cloned.1.call-start = ((), (), s32[]{:S(2)}) async-start(), calls=%async_computation.25 | async-start | bytes 2359296 | tf_op jit(solution)/shard_map/all_gather | solution.py:52
  159.9 21.2 %collective-permute-start.1 = (bf16[256,1536]{1,0:T(8,128)(2,1)}, bf16[256,1536]{1,0:T(8,128)(2,1)}, u32[]{:S(2)}, u32[]{:S(2)}) collective-permute-start(bf16[256,1536]{1,0:T(8,128)(2,1)} %get-tuple-element.46), channel_id=1, source_target_pairs={{0,16},{1,17},{2,18},{3,19},{4,20},{5,21},{6,22},{7,23},{8,24},{9,... | collective-permute-start | bytes 2359304 | tf_op jit(solution)/shard_map/ppermute | solution.py:14
  196.4 67.7 %all-reduce.7.cloned.1.call-start = ((), (), s32[]{:S(2)}) async-start(), calls=%async_computation.8 | async-start | bytes 1572864 | tf_op jit(solution)/shard_map/psum | solution.py:58
  243.6 46.7 %all-gather.23.cloned.1.call-start = ((), (), s32[]{:S(2)}) async-start(), calls=%async_computation.26 | async-start | bytes 2359296 | tf_op jit(solution)/shard_map/all_gather | solution.py:52
  250.1 56.9 %all-reduce.9.cloned.1.call-start = ((), (), s32[]{:S(2)}) async-start(), calls=%async_computation.9 | async-start | bytes 1572864 | tf_op jit(solution)/shard_map/psum | solution.py:58
  286.6 79.6 %all-reduce.11.cloned.1.call-start = ((), (), s32[]{:S(2)}) async-start(), calls=%async_computation.10 | async-start | bytes 1572864 | tf_op jit(solution)/shard_map/psum | solution.py:58
  309.5 32.5 %slice-start.12 = ((s8[6291456]{0:T(1024)(128)(4,1)}), s8[4194304]{0:T(1024)(128)(4,1)S(1)}, s32[]{:S(2)}) async-start(s8[6291456]{0:T(1024)(128)(4,1)} %bitcast.962), calls=%async_computation.40 | async-start | bytes 8388608
  309.6 34.4 %slice-start.14 = ((s8[6291456]{0:T(1024)(128)(4,1)}), s8[4194304]{0:T(1024)(128)(4,1)S(1)}, s32[]{:S(2)}) async-start(s8[6291456]{0:T(1024)(128)(4,1)} %bitcast.964), calls=%async_computation.42 | async-start | bytes 8388608
  313.6 28.5 %copy-start.69 = (bf16[256,1536]{1,0:T(8,128)(2,1)}, bf16[256,1536]{1,0:T(8,128)(2,1)S(1)}, u32[]{:S(2)}) copy-start(bf16[256,1536]{1,0:T(8,128)(2,1)S(1)} %get-tuple-element.76) | copy-start | bytes 2359300
  313.6 21.7 %collective-permute-start.2 = (bf16[256,1536]{1,0:T(8,128)(2,1)S(1)}, bf16[256,1536]{1,0:T(8,128)(2,1)S(1)}, u32[]{:S(2)}, u32[]{:S(2)}) collective-permute-start(bf16[256,1536]{1,0:T(8,128)(2,1)S(1)} %get-tuple-element.76), channel_id=1, source_target_pairs={{16,0},{17,1},{18,2},{19,3},{20,4},{21,5},{22,6},{23,7},{24,8},{25... | collective-permute-start | bytes 2359304 | tf_op jit(solution)/shard_map/ppermute | solution.py:14
  335.4 33.6 %copy-start.39 = (bf16[256,1536]{1,0:T(8,128)(2,1)}, bf16[256,1536]{1,0:T(8,128)(2,1)S(1)}, u32[]{:S(2)}) copy-start(bf16[256,1536]{1,0:T(8,128)(2,1)S(1)} %bitcast_select_fusion.1) | copy-start | bytes 2359300
  346.7 60.0 %all-reduce.13.cloned.1.call-start = ((), (), s32[]{:S(2)}) async-start(), calls=%async_computation.11 | async-start | bytes 1572864 | tf_op jit(solution)/shard_map/psum | solution.py:58
  386.4 86.1 %all-reduce.15.cloned.1.call-start = ((), (), s32[]{:S(2)}) async-start(), calls=%async_computation.12 | async-start | bytes 1572864 | tf_op jit(solution)/shard_map/psum | solution.py:58
  412.1 21.9 %collective-permute-start.3 = (bf16[256,1536]{1,0:T(8,128)(2,1)}, bf16[256,1536]{1,0:T(8,128)(2,1)}, u32[]{:S(2)}, u32[]{:S(2)}) collective-permute-start(bf16[256,1536]{1,0:T(8,128)(2,1)} %fusion.169), channel_id=1, source_target_pairs={{16,0},{17,1},{18,2},{19,3},{20,4},{21,5},{22,6},{23,7},{24,8},{25... | collective-permute-start | bytes 2359304 | tf_op jit(solution)/shard_map/ppermute | solution.py:14
  453.0 61.7 %all-reduce.17.cloned.1.call-start = ((), (), s32[]{:S(2)}) async-start(), calls=%async_computation.13 | async-start | bytes 1572864 | tf_op jit(solution)/shard_map/psum | solution.py:58
  494.4 140.1 %reduce-scatter.25.cloned.1.call-start = ((), (), s32[]{:S(2)}) async-start(), calls=%async_computation.27 | async-start | bytes 442368
  518.2 131.0 %reduce-scatter.13.cloned.1.call-start = ((), (), s32[]{:S(2)}) async-start(), calls=%async_computation.15 | async-start | bytes 1327104 | tf_op jit(solution)/shard_map/reduce_scatter | solution.py:321
  521.9 194.4 %reduce-scatter.15.cloned.1.call-start = ((), (), s32[]{:S(2)}) async-start(), calls=%async_computation.16 | async-start | bytes 1327104 | tf_op jit(solution)/shard_map/reduce_scatter | solution.py:324
  526.5 261.8 %reduce-scatter.11.cloned.1.call-start = ((), (), s32[]{:S(2)}) async-start(), calls=%async_computation.14 | async-start | bytes 2654208 | tf_op jit(solution)/shard_map/reduce_scatter | solution.py:318
  532.6 327.9 %reduce-scatter.17.cloned.1.call-start = ((), (), s32[]{:S(2)}) async-start(), calls=%async_computation.17 | async-start | bytes 2654208 | tf_op jit(solution)/shard_map/reduce_scatter | solution.py:327
  540.2 441.1 %reduce-scatter.19.cloned.1.call-start = ((), (), s32[]{:S(2)}) async-start(), calls=%async_computation.18 | async-start | bytes 7077888 | tf_op jit(solution)/shard_map/reduce_scatter | solution.py:330
  568.5 533.6 %reduce-scatter.21.cloned.1.call-start = ((), (), s32[]{:S(2)}) async-start(), calls=%async_computation.19 | async-start | bytes 7077888 | tf_op jit(solution)/shard_map/reduce_scatter | solution.py:333
  596.4 626.5 %reduce-scatter.23.cloned.1.call-start = ((), (), s32[]{:S(2)}) async-start(), calls=%async_computation.20 | async-start | bytes 7077888 | tf_op jit(solution)/shard_map/reduce_scatter | solution.py:336
  (184 other events, 774.6 us)
Sparse Core Ops, SparseCore 0:
  32.5 12.5 all-gather.12
  61.2 10.9 all-gather.14
  112.9 11.7 all-gather.16
  143.1 10.9 all-gather.18
  196.6 11.9 all-gather.20
  243.7 20.3 all-reduce.6
  265.7 10.9 all-gather.22
  286.7 20.2 all-reduce.8
  346.9 19.2 all-reduce.10
  386.5 20.1 all-reduce.12
  453.2 19.2 all-reduce.14
  494.6 20.1 all-reduce.16
  518.6 63.3 reduce-scatter.24
  585.2 63.9 reduce-scatter.12
  652.4 63.8 reduce-scatter.14
  719.7 68.5 reduce-scatter.10
  791.6 68.8 reduce-scatter.16
  864.0 117.2 reduce-scatter.18
  984.8 117.2 reduce-scatter.20
  1105.6 117.2 reduce-scatter.22
